TPU v7x, 32 devices: a whole 2x2x4 slice. The times are simulated.
32 devices in a mesh: groups: 2 (over y), col: 16 (over z, x, core).
Axes of the slice: x: 2, y: 2, z: 4, core: 2. Of those that a mesh axis runs over, the one named last changes fastest.
Arguments:
- fields: bfloat16 [32, 137, 2048], P(('groups', 'col')), parts along dimension 0, may hold values from -6 to 6
- level_count: int32 [2048], replicated, may hold values from 68 to 137
- owner: int32 [16], replicated, may hold values from 0 to 15, as said below
- band_start: int32 [16, 37], replicated, may hold values from 0 to 133
- interp_weights: float32 [16, 37, 4], replicated, may hold values from -3 to 3
Outputs:
- timemajor: bfloat16 [32, 37, 2048], P(('groups', 'col')), parts along dimension 0
- series: bfloat16 [96, 37, 16, 128], P(('groups', 'col')), parts along dimension 0
There are 2 independent parts, one for each index of `groups`. A program takes and returns all parts, laid end to end along the dimension named above; an argument that names none is the same for every part. Nothing has to cross between parts.
Inputs may be any that keep to these rules, and one draw needn't show every extreme that they name: No owner holds more than 3 blocks, and some owner holds exactly 3.
All inputs are finite; a program needn't handle non-finite values.
Results may differ from a plain program's by a relative error of at most 0.0085.
Values may be sent and summed in bfloat16 or wider, within the bound.
A program may use at most 64 MiB of HBM per device.

v0:
```python
import jax
import jax.numpy as jnp
from jax import lax
from jax.sharding import PartitionSpec as P

LEV = 137
PLEV = 37
BAND = 4
CBLK = 128
MOST = 3


def slot_tables(owner, devices):
    blocks = owner.shape[0]
    onehot = (owner[:, None] == jnp.arange(devices, dtype=jnp.int32)[None, :]).astype(jnp.int32)
    before = jnp.cumsum(onehot, axis=0) - onehot
    slot = jnp.sum(before * onehot, axis=1)
    global_slot = owner * MOST + slot
    hit = global_slot[:, None] == jnp.arange(devices * MOST, dtype=jnp.int32)[None, :]
    block_of = jnp.sum(jnp.where(hit, jnp.arange(blocks, dtype=jnp.int32)[:, None], 0), axis=0)
    occupied = jnp.any(hit, axis=0)
    return (global_slot, block_of, occupied)


def fill_levels(data, counts):
    lev = jnp.arange(LEV, dtype=jnp.int32)[None, :, None, None]
    wanted = counts[None, None, :, :]
    last = jnp.sum(
        jnp.where(lev == wanted - 1, data.astype(jnp.float32), 0.0), axis=1, keepdims=True
    )
    return jnp.where(lev < wanted, data, last.astype(jnp.bfloat16))


def level_matrices(weights, starts):
    lev = jnp.arange(LEV, dtype=jnp.int32)
    offsets = jnp.arange(BAND, dtype=jnp.int32)
    hit = lev[None, None, None, :] == (starts[:, :, None] + offsets[None, None, :])[:, :, :, None]
    return jnp.sum(weights[:, :, :, None] * hit.astype(jnp.float32), axis=2).astype(jnp.bfloat16)


def pack_slots(data, block_of, occupied, devices):
    taken = jnp.take(data, block_of, axis=2)
    taken = jnp.where(occupied[None, None, :, None], taken, jnp.zeros((), data.dtype))
    return taken.reshape(data.shape[0], data.shape[1], devices, MOST, data.shape[3])


def per_device(fields, level_count, owner, band_start, interp_weights):
    devices = lax.axis_size("col")
    blocks = owner.shape[0]
    steps_here = fields.shape[0]
    global_slot, block_of, occupied = slot_tables(owner, devices)
    grouped = fields.reshape(steps_here, LEV, blocks, CBLK)
    counts = level_count.reshape(blocks, CBLK)
    filled = fill_levels(grouped, counts)
    matrices = level_matrices(interp_weights, band_start)
    result = jnp.einsum(
        "bpl,tlbc->tpbc", matrices, filled, preferred_element_type=jnp.float32
    ).astype(jnp.bfloat16)
    timemajor = result.reshape(steps_here, PLEV, blocks * CBLK)
    packed = pack_slots(result, block_of, occupied, devices)
    arrived = lax.all_to_all(packed, "col", split_axis=2, concat_axis=0, tiled=True)
    arrived = arrived.reshape(devices * steps_here, PLEV, MOST, CBLK)
    series = jnp.transpose(arrived, (2, 1, 0, 3))
    return (timemajor, series)


def solution(mesh):
    placed = (P(("groups", "col"), None, None), P(), P(), P(), P())
    return jax.shard_map(
        per_device,
        mesh=mesh,
        in_specs=placed,
        out_specs=(P(("groups", "col"), None, None), P(("groups", "col"), None, None, None)),
        check_vma=False,
    )
```

profile of v0, /device:TPU:0, one launch (start us, length us, event | category | flops | bytes accessed | tf_op | source)
XLA Modules:
  0.0 30.6 jit_solution(929078646718068215)
XLA Ops:
  0.6 0.7 %fusion.7 = s32[16,16]{1,0:T(8,128)S(1)} fusion(s32[16]{0:T(128)} %param.7), kind=kLoop, calls=%fused_computation.20 | loop fusion | flops 512 | bytes 1088 | tf_op jit(solution)/shard_map/convert_element_type | solution.py:15
  1.4 0.8 %select_reduce_fusion.3 = s32[16]{0:T(128)S(1)} fusion(s32[16,16]{1,0:T(8,128)S(1)} %reduce_window_sum.11, s32[16]{0:T(128)} %param.7), kind=kLoop, calls=%fused_computation.18 | loop fusion | flops 1264 | bytes 1152 | tf_op jit(solution)/shard_map/reduce_sum | solution.py:17
  2.2 0.7 %multiply_add_fusion = s32[16]{0:T(128)S(1)} fusion(s32[16]{0:T(128)S(1)} %select_reduce_fusion.3, s32[16]{0:T(128)} %param.7), kind=kLoop, calls=%fused_computation.27 | loop fusion | flops 32 | bytes 192 | tf_op jit(solution)/shard_map/add | solution.py:18
  2.9 0.1 select_reduce_fusion.2
  3.0 0.1 reduce_sum.44
  3.1 0.1 fusion.6
  3.2 1.2 %copy.30 = bf16[18,8,16,128]{3,2,1,0:T(8,128)(2,1)S(1)} copy(bf16[18,8,16,128]{3,1,2,0:T(8,128)(2,1)} %bitcast.31) | data formatting | bytes 1179648
  4.4 0.0 copy-start.1
  4.4 0.0 copy-start.2
  4.4 0.0 copy-start.3
  4.4 0.0 copy-start
  4.4 0.1 slice.2
  4.5 0.6 %copy-done.1 = f32[16,37,4]{1,2,0:T(4,128)S(1)} copy-done((f32[16,37,4]{1,2,0:T(4,128)S(1)}, f32[16,37,4]{1,2,0:T(4,128)}, u32[]{:S(2)}) %copy-start.1) | copy-done | bytes 9496
  5.1 0.1 copy.25
  5.2 0.0 copy-done.2
  5.2 0.1 copy.24
  5.3 0.0 copy-done.3
  5.4 0.1 copy-done
  5.5 0.2 select_reduce_fusion.1
  5.7 0.1 broadcast_in_dim.63
  5.8 0.9 %select_reduce_fusion = bf16[16,37,137]{2,0,1:T(8,128)(2,1)S(1)} fusion(f32[16,37,4]{0,2,1:T(4,128)S(1)} %copy.25, s32[16,37,4]{0,2,1:T(4,128)S(1)} %iota_add_fusion), kind=kLoop, calls=%fused_computation.1 | loop fusion | flops 892144 | bytes 181152 | tf_op jit(solution)/shard_map/reduce_sum | solution.py:38
  6.7 0.3 %convolution_convert_fusion = bf16[16,128,37]{1,2,0:T(8,128)(2,1)S(1)} fusion(bf16[137,16,128]{2,1,0:T(8,128)(2,1)S(1)} %slice.2, s32[16,128]{1,0:T(8,128)S(1)} %bitcast.37, bf16[16,37,137]{2,0,1:T(8,128)(2,1)S(1)} %select_reduce_fusion, bf16[16,128]{1,0:T(8,128)(2,1)S(1)} %bitcast.38), kind=kOutput, calls=%fused_computation.7 | convolution fusion | flops 21399552 | bytes 887200 | tf_op jit(solution)/shard_map/bpl,tlbc->tpbc/dot_general | solution.py:56
  7.0 0.7 %gather_fusion = bf16[48,37,128]{2,1,0:T(8,128)(2,1)S(1)} fusion(bf16[37,16,128]{2,0,1:T(8,128)(2,1)S(1)} %bitcast.32, s32[1024]{0:T(1024)S(1)} %pad_clamp_fusion), kind=kCustom, calls=%fused_computation | custom fusion | bytes 909504 | tf_op jit(solution)/shard_map/jit(_take)/gather | solution.py:42
  7.7 0.9 %select_select_fusion = bf16[1,37,16,3,128]{4,1,3,0,2:T(8,128)(2,1)} fusion(bf16[1,37,16,3,128]{4,1,3,0,2:T(8,128)(2,1)S(1)} %bitcast.36, pred[16,3]{1,0:T(8,128)(4,1)S(1)} %compare_and_fusion, pred[16,3]{1,0:T(8,128)(4,1)S(1)} %broadcast_in_dim.63), kind=kLoop, calls=%fused_computation.10 | loop fusion | flops 454656 | bytes 909408 | tf_op jit(solution)/shard_map/jit(_where)/select_n | solution.py:43
  8.6 7.4 %all-to-all-start = ((bf16[1,37,16,3,128]{4,1,3,0,2:T(8,128)(2,1)}), bf16[1,37,16,3,128]{4,1,3,0,2:T(8,128)(2,1)S(1)}, u32[]{:S(2)}, u32[]{:S(2)}) async-start(bf16[1,37,16,3,128]{4,1,3,0,2:T(8,128)(2,1)} %select_select_fusion), calls=%async_computation | async-start | bytes 983040 | tf_op jit(solution)/shard_map/all_to_all | solution.py:61
  16.1 0.8 %reshape.127 = bf16[1,37,2048]{2,1,0:T(8,128)(2,1)} reshape(bf16[1,37,16,128]{3,2,1,0:T(8,128)(2,1)S(1)} %copy.27) | data formatting | bytes 303104 | tf_op jit(solution)/shard_map/reshape | solution.py:59
  16.8 12.9 %all-to-all-done = bf16[1,37,16,3,128]{4,1,3,0,2:T(8,128)(2,1)S(1)} async-done(((bf16[1,37,16,3,128]{4,1,3,0,2:T(8,128)(2,1)}), bf16[1,37,16,3,128]{4,1,3,0,2:T(8,128)(2,1)S(1)}, u32[]{:S(2)}, u32[]{:S(2)}) %all-to-all-start) | async-done | bytes 454688 | tf_op jit(solution)/shard_map/all_to_all | solution.py:61
  29.8 0.8 %copy.29 = bf16[3,37,16,128]{3,2,1,0:T(8,128)(2,1)} copy(bf16[3,37,16,128]{3,1,0,2:T(8,128)(2,1)S(1)} %bitcast.35) | data formatting | bytes 909312
  (7 shorter events, 0.1 us)
Async XLA Ops:
  4.4 0.8 %copy-start.1 = (f32[16,37,4]{1,2,0:T(4,128)S(1)}, f32[16,37,4]{1,2,0:T(4,128)}, u32[]{:S(2)}) copy-start(f32[16,37,4]{1,2,0:T(4,128)} %param.9) | copy-start | bytes 28420
  4.4 0.9 %copy-start.2 = (s32[16,37]{1,0:T(8,128)S(1)}, s32[16,37]{1,0:T(8,128)}, u32[]{:S(2)}) copy-start(s32[16,37]{1,0:T(8,128)} %param.8) | copy-start | bytes 7108
  4.4 1.0 %copy-start.3 = (s32[2048]{0:T(1024)S(1)}, s32[2048]{0:T(1024)}, u32[]{:S(2)}) copy-start(s32[2048]{0:T(1024)} %param.6) | copy-start | bytes 24580
  4.4 1.1 %copy-start = (bf16[1,137,2048]{2,1,0:T(8,128)(2,1)S(1)}, bf16[1,137,2048]{2,1,0:T(8,128)(2,1)}, u32[]{:S(2)}) copy-start(bf16[1,137,2048]{2,1,0:T(8,128)(2,1)} %param.5) | copy-start | bytes 1683460
  8.6 21.1 %all-to-all-start = ((bf16[1,37,16,3,128]{4,1,3,0,2:T(8,128)(2,1)}), bf16[1,37,16,3,128]{4,1,3,0,2:T(8,128)(2,1)S(1)}, u32[]{:S(2)}, u32[]{:S(2)}) async-start(bf16[1,37,16,3,128]{4,1,3,0,2:T(8,128)(2,1)} %select_select_fusion), calls=%async_computation | async-start | bytes 983040 | tf_op jit(solution)/shard_map/all_to_all | solution.py:61
where the time goes:
time: 30.9 us; the launch traced here: 30.6 us
  waiting for transfers between devices  12.9 us (42%)
  starting transfers between devices  7.39 us (24%)
  local copies, waits for them, and re-layouts  4.66 us (15%)
  other arithmetic  4.52 us (15%)
  between operations  0.76 us (2%)
  matrix products  0.34 us (1%)
    all_to_all x1, waiting for transfers between devices, per_device(): lax.all_to_all(packed, 'col', split_axis=2, concat_axis=0, tiled=True)  12.9 us
    all_to_all x1, starting transfers between devices, per_device(): lax.all_to_all(packed, 'col', split_axis=2, concat_axis=0, tiled=True)  7.39 us
    unnamed x12, local copies, waits for them, and re-layouts  2.94 us
    select_n x1, other arithmetic, pack_slots(): jnp.where(occupied[None, None, :, None], taken, jnp.zeros((), data.dtype))  0.95 us
    reduce_sum x1, other arithmetic, level_matrices(): jnp.sum(weights[:, :, :, None] * hit.astype(jnp.float32), axis=2)  0.9 us
    reduce_sum x1, other arithmetic, slot_tables(): slot = jnp.sum(before * onehot, axis=1)  0.84 us
    reshape x1, local copies, waits for them, and re-layouts, per_device(): timemajor = result.reshape(steps_here, PLEV, blocks * CBLK)  0.76 us
    convert_element_type x1, other arithmetic, slot_tables(): (owner[:, None] == jnp.arange(devices, dtype=jnp.int32)[None, :]).astype(...  0.73 us
  transfers between devices with their start and end apart: 1, of which 1 were waited for; matrix products, arithmetic and copies ran while one was open for 3% of the time, Pallas kernels for 0%

commit v1 on v0

--- a/solution.py
+++ b/solution.py
@@ -58,7 +58,10 @@
     ).astype(jnp.bfloat16)
     timemajor = result.reshape(steps_here, PLEV, blocks * CBLK)
     packed = pack_slots(result, block_of, occupied, devices)
-    arrived = lax.all_to_all(packed, "col", split_axis=2, concat_axis=0, tiled=True)
+    arrived = jnp.concatenate(
+        lax.all_to_all(jnp.stack(jnp.split(packed, lax.axis_size("col"), axis=2)), "col", 0, 0),
+        axis=0,
+    )
     arrived = arrived.reshape(devices * steps_here, PLEV, MOST, CBLK)
     series = jnp.transpose(arrived, (2, 1, 0, 3))
     return (timemajor, series)

time: 30.9 us -> 41.5 us (1.34)
  local copies, waits for them, and re-layouts: 4.66 us -> 14 us
  other arithmetic: 4.52 us -> 5.59 us
    unnamed x12 -> x23, local copies, waits for them, and re-layouts: 2.94 us -> 11.7 us
    reduce_sum x1, other arithmetic: 0.19 us -> 1.26 us  [fill_levels(): jnp.sum(jnp.where(lev == wanted - 1, data.astype(jnp.float32), 0.0), axis...]
    select_n x1, other arithmetic: 0.95 us -> 0.17 us  [pack_slots(): jnp.where(occupied[None, None, :, None], taken, jnp.zeros((), data.dtype))]
    sub x1, other arithmetic: 0.01 us -> 0.71 us  [fill_levels(): wanted - 1]
    another operation x0 -> x1, local copies, waits for them, and re-layouts: none -> 0.6 us  [per_device(): jnp.stack(jnp.split(packed, lax.axis_size('col'), axis=2))]
  transfers between devices with their start and end apart: 1 -> 1, of which waited for: 1 -> 1; matrix products, arithmetic and copies ran while one was open for 3% -> 2% of each run, Pallas kernels for 0% -> 0%
where the time goes in v1:
time: 41.5 us; the launch traced here: 41.1 us
  local copies, waits for them, and re-layouts  14 us (34%)
  waiting for transfers between devices  12.9 us (31%)
  starting transfers between devices  7.39 us (18%)
  other arithmetic  5.59 us (13%)
  between operations  0.75 us (2%)
    all_to_all x1, waiting for transfers between devices, per_device(): lax.all_to_all(jnp.stack(jnp.split(packed, lax.axis_size('col'), axis=2))...  12.9 us
    unnamed x23, local copies, waits for them, and re-layouts  11.7 us
    all_to_all x1, starting transfers between devices, per_device(): lax.all_to_all(jnp.stack(jnp.split(packed, lax.axis_size('col'), axis=2))...  7.39 us
    reduce_sum x1, other arithmetic, fill_levels(): jnp.sum(jnp.where(lev == wanted - 1, data.astype(jnp.float32), 0.0), axis...  1.26 us
    reduce_sum x1, other arithmetic, level_matrices(): jnp.sum(weights[:, :, :, None] * hit.astype(jnp.float32), axis=2)  0.91 us
    reduce_sum x1, other arithmetic, slot_tables(): slot = jnp.sum(before * onehot, axis=1)  0.84 us
  transfers between devices with their start and end apart: 1, of which 1 were waited for; matrix products, arithmetic and copies ran while one was open for 2% of the time, Pallas kernels for 0%

profile of v1, /device:TPU:0, one launch (start us, length us, event | category | flops | bytes accessed | tf_op | source)
XLA Modules:
  0.0 41.1 jit_solution(13154888374146993948)
XLA Ops:
  0.6 0.0 copy-start
  0.6 0.8 %fusion.7 = s32[16,16]{1,0:T(8,128)S(1)} fusion(s32[16]{0:T(128)} %param.7), kind=kLoop, calls=%fused_computation.52 | loop fusion | flops 512 | bytes 1088 | tf_op jit(solution)/shard_map/convert_element_type | solution.py:15
  1.5 0.8 %select_reduce_fusion.3 = s32[16]{0:T(128)S(1)} fusion(s32[16,16]{1,0:T(8,128)S(1)} %reduce_window_sum.11, s32[16]{0:T(128)} %param.7), kind=kLoop, calls=%fused_computation.50 | loop fusion | flops 1264 | bytes 1152 | tf_op jit(solution)/shard_map/reduce_sum | solution.py:17
  2.3 0.7 %multiply_add_fusion = s32[16]{0:T(128)S(1)} fusion(s32[16]{0:T(128)S(1)} %select_reduce_fusion.3, s32[16]{0:T(128)} %param.7), kind=kLoop, calls=%fused_computation.59 | loop fusion | flops 32 | bytes 192 | tf_op jit(solution)/shard_map/add | solution.py:18
  3.0 0.1 select_reduce_fusion.2
  3.1 0.1 fusion.6
  3.2 0.1 reduce_sum.44
  3.2 0.7 %broadcast_add_fusion = s32[2048]{0:T(1024)S(1)} fusion(s32[2048]{0:T(1024)} %param.6), kind=kLoop, calls=%fused_computation.56 | loop fusion | flops 2048 | bytes 16384 | tf_op jit(solution)/shard_map/sub | solution.py:29
  3.9 0.1 broadcast_in_dim.63
  4.1 0.8 %copy.29 = s32[16,37]{0,1:T(8,128)S(1)} copy(s32[16,37]{1,0:T(8,128)} %param.8) | data formatting | bytes 4736 | tf_op args[3]
  4.9 0.9 %copy.30 = f32[16,37,4]{0,2,1:T(4,128)S(1)} copy(f32[16,37,4]{1,2,0:T(4,128)} %param.9) | data formatting | bytes 18944 | tf_op args[4]
  5.7 1.3 %select_reduce_fusion.1 = bf16[2048]{0:T(1024)(128)(2,1)S(1)} fusion(bf16[1,137,2048]{2,1,0:T(8,128)(2,1)} %param.5, s32[2048]{0:T(1024)S(1)} %broadcast_add_fusion), kind=kLoop, calls=%fused_computation.3 | loop fusion | flops 1120256 | bytes 573440 | tf_op jit(solution)/shard_map/reduce_sum | solution.py:28
  7.0 0.0 copy-done
  7.0 0.1 copy.34
  7.1 0.0 copy-start.1
  7.1 0.1 slice.2
  7.2 0.9 %select_reduce_fusion = bf16[16,37,137]{2,0,1:T(8,128)(2,1)S(1)} fusion(f32[16,37,4]{0,2,1:T(4,128)S(1)} %copy.30, s32[16,37,4]{0,2,1:T(4,128)S(1)} %iota_add_fusion), kind=kLoop, calls=%fused_computation.1 | loop fusion | flops 892144 | bytes 181152 | tf_op jit(solution)/shard_map/reduce_sum | solution.py:38
  8.1 0.0 copy-done.1
  8.2 0.3 convolution_convert_fusion
  8.5 0.7 %gather_fusion = bf16[48,37,128]{2,1,0:T(8,128)(2,1)S(1)} fusion(bf16[37,16,128]{2,0,1:T(8,128)(2,1)S(1)} %bitcast.90, s32[1024]{0:T(1024)S(1)} %pad_clamp_fusion), kind=kCustom, calls=%fused_computation | custom fusion | bytes 909504 | tf_op jit(solution)/shard_map/jit(_take)/gather | solution.py:42
  9.2 0.2 select_select_fusion
  9.3 0.6 %constant_dynamic-update-slice_fusion.15 = bf16[16,1,37,1,3,128]{5,2,4,3,1,0:T(8,128)(2,1)} fusion(bf16[1,37,16,3,128]{4,1,3,2,0:T(8,128)(2,1)S(1)} %select_select_fusion), kind=kLoop, calls=%fused_computation.29 | loop fusion | bytes 59136
  10.0 0.6 %constant_dynamic-update-slice_fusion.14 = bf16[16,1,37,1,3,128]{5,2,4,3,1,0:T(8,128)(2,1)} fusion(bf16[16,1,37,1,3,128]{5,2,4,3,1,0:T(8,128)(2,1)} %constant_dynamic-update-slice_fusion.15, bf16[1,37,16,3,128]{4,1,3,2,0:T(8,128)(2,1)S(1)} %select_select_fusion), kind=kLoop, calls=%fused_computation.28 | loop fusion | bytes 59136
  10.6 0.6 %constant_dynamic-update-slice_fusion.13 = bf16[16,1,37,1,3,128]{5,2,4,3,1,0:T(8,128)(2,1)} fusion(bf16[16,1,37,1,3,128]{5,2,4,3,1,0:T(8,128)(2,1)} %constant_dynamic-update-slice_fusion.14, bf16[1,37,16,3,128]{4,1,3,2,0:T(8,128)(2,1)S(1)} %select_select_fusion), kind=kLoop, calls=%fused_computation.27 | loop fusion | bytes 59136
  11.2 0.6 %constant_dynamic-update-slice_fusion.12 = bf16[16,1,37,1,3,128]{5,2,4,3,1,0:T(8,128)(2,1)} fusion(bf16[16,1,37,1,3,128]{5,2,4,3,1,0:T(8,128)(2,1)} %constant_dynamic-update-slice_fusion.13, bf16[1,37,16,3,128]{4,1,3,2,0:T(8,128)(2,1)S(1)} %select_select_fusion), kind=kLoop, calls=%fused_computation.26 | loop fusion | bytes 59136
  11.8 0.6 %constant_dynamic-update-slice_fusion.11 = bf16[16,1,37,1,3,128]{5,2,4,3,1,0:T(8,128)(2,1)} fusion(bf16[16,1,37,1,3,128]{5,2,4,3,1,0:T(8,128)(2,1)} %constant_dynamic-update-slice_fusion.12, bf16[1,37,16,3,128]{4,1,3,2,0:T(8,128)(2,1)S(1)} %select_select_fusion), kind=kLoop, calls=%fused_computation.25 | loop fusion | bytes 59136
  12.4 0.6 %constant_dynamic-update-slice_fusion.10 = bf16[16,1,37,1,3,128]{5,2,4,3,1,0:T(8,128)(2,1)} fusion(bf16[16,1,37,1,3,128]{5,2,4,3,1,0:T(8,128)(2,1)} %constant_dynamic-update-slice_fusion.11, bf16[1,37,16,3,128]{4,1,3,2,0:T(8,128)(2,1)S(1)} %select_select_fusion), kind=kLoop, calls=%fused_computation.24 | loop fusion | bytes 59136
  13.0 0.6 %constant_dynamic-update-slice_fusion.9 = bf16[16,1,37,1,3,128]{5,2,4,3,1,0:T(8,128)(2,1)} fusion(bf16[16,1,37,1,3,128]{5,2,4,3,1,0:T(8,128)(2,1)} %constant_dynamic-update-slice_fusion.10, bf16[1,37,16,3,128]{4,1,3,2,0:T(8,128)(2,1)S(1)} %select_select_fusion), kind=kLoop, calls=%fused_computation.23 | loop fusion | bytes 59136
  13.6 0.6 %constant_dynamic-update-slice_fusion.8 = bf16[16,1,37,1,3,128]{5,2,4,3,1,0:T(8,128)(2,1)} fusion(bf16[16,1,37,1,3,128]{5,2,4,3,1,0:T(8,128)(2,1)} %constant_dynamic-update-slice_fusion.9, bf16[1,37,16,3,128]{4,1,3,2,0:T(8,128)(2,1)S(1)} %select_select_fusion), kind=kLoop, calls=%fused_computation.22 | loop fusion | bytes 59136
  14.2 0.6 %constant_dynamic-update-slice_fusion.7 = bf16[16,1,37,1,3,128]{5,2,4,3,1,0:T(8,128)(2,1)} fusion(bf16[16,1,37,1,3,128]{5,2,4,3,1,0:T(8,128)(2,1)} %constant_dynamic-update-slice_fusion.8, bf16[1,37,16,3,128]{4,1,3,2,0:T(8,128)(2,1)S(1)} %select_select_fusion), kind=kLoop, calls=%fused_computation.21 | loop fusion | bytes 59136
  14.8 0.6 %constant_dynamic-update-slice_fusion.6 = bf16[16,1,37,1,3,128]{5,2,4,3,1,0:T(8,128)(2,1)} fusion(bf16[16,1,37,1,3,128]{5,2,4,3,1,0:T(8,128)(2,1)} %constant_dynamic-update-slice_fusion.7, bf16[1,37,16,3,128]{4,1,3,2,0:T(8,128)(2,1)S(1)} %select_select_fusion), kind=kLoop, calls=%fused_computation.20 | loop fusion | bytes 59136
  15.4 0.6 %constant_dynamic-update-slice_fusion.5 = bf16[16,1,37,1,3,128]{5,2,4,3,1,0:T(8,128)(2,1)} fusion(bf16[16,1,37,1,3,128]{5,2,4,3,1,0:T(8,128)(2,1)} %constant_dynamic-update-slice_fusion.6, bf16[1,37,16,3,128]{4,1,3,2,0:T(8,128)(2,1)S(1)} %select_select_fusion), kind=kLoop, calls=%fused_computation.19 | loop fusion | bytes 59136
  16.1 0.6 %constant_dynamic-update-slice_fusion.4 = bf16[16,1,37,1,3,128]{5,2,4,3,1,0:T(8,128)(2,1)} fusion(bf16[16,1,37,1,3,128]{5,2,4,3,1,0:T(8,128)(2,1)} %constant_dynamic-update-slice_fusion.5, bf16[1,37,16,3,128]{4,1,3,2,0:T(8,128)(2,1)S(1)} %select_select_fusion), kind=kLoop, calls=%fused_computation.18 | loop fusion | bytes 59136
  16.7 0.6 %constant_dynamic-update-slice_fusion.3 = bf16[16,1,37,1,3,128]{5,2,4,3,1,0:T(8,128)(2,1)} fusion(bf16[16,1,37,1,3,128]{5,2,4,3,1,0:T(8,128)(2,1)} %constant_dynamic-update-slice_fusion.4, bf16[1,37,16,3,128]{4,1,3,2,0:T(8,128)(2,1)S(1)} %select_select_fusion), kind=kLoop, calls=%fused_computation.17 | loop fusion | bytes 59136
  17.3 0.6 %constant_dynamic-update-slice_fusion.2 = bf16[16,1,37,1,3,128]{5,2,4,3,1,0:T(8,128)(2,1)} fusion(bf16[16,1,37,1,3,128]{5,2,4,3,1,0:T(8,128)(2,1)} %constant_dynamic-update-slice_fusion.3, bf16[1,37,16,3,128]{4,1,3,2,0:T(8,128)(2,1)S(1)} %select_select_fusion), kind=kLoop, calls=%fused_computation.16 | loop fusion | bytes 59136
  17.9 0.6 %constant_dynamic-update-slice_fusion.1 = bf16[16,1,37,1,3,128]{5,2,4,3,1,0:T(8,128)(2,1)} fusion(bf16[16,1,37,1,3,128]{5,2,4,3,1,0:T(8,128)(2,1)} %constant_dynamic-update-slice_fusion.2, bf16[1,37,16,3,128]{4,1,3,2,0:T(8,128)(2,1)S(1)} %select_select_fusion), kind=kLoop, calls=%fused_computation.15 | loop fusion | bytes 59136
  18.5 0.6 %constant_dynamic-update-slice_fusion = bf16[16,1,37,1,3,128]{5,2,4,3,1,0:T(8,128)(2,1)} fusion(bf16[16,1,37,1,3,128]{5,2,4,3,1,0:T(8,128)(2,1)} %constant_dynamic-update-slice_fusion.1, bf16[1,37,16,3,128]{4,1,3,2,0:T(8,128)(2,1)S(1)} %select_select_fusion), kind=kLoop, calls=%fused_computation.14 | loop fusion | bytes 59136 | tf_op jit(solution)/shard_map/stack | solution.py:62
  19.1 7.4 %all-to-all-start = ((bf16[16,1,37,1,3,128]{5,2,4,3,1,0:T(8,128)(2,1)}), bf16[16,1,37,1,3,128]{5,2,4,3,1,0:T(8,128)(2,1)S(1)}, u32[]{:S(2)}, u32[]{:S(2)}) async-start(bf16[16,1,37,1,3,128]{5,2,4,3,1,0:T(8,128)(2,1)} %constant_dynamic-update-slice_fusion), calls=%async_computation | async-start | bytes 983040 | tf_op jit(solution)/shard_map/all_to_all | solution.py:62
  26.5 0.8 %reshape.123 = bf16[1,37,2048]{2,1,0:T(8,128)(2,1)} reshape(bf16[1,37,16,128]{3,2,1,0:T(8,128)(2,1)S(1)} %copy.32) | data formatting | bytes 303104 | tf_op jit(solution)/shard_map/reshape | solution.py:59
  27.3 12.9 %all-to-all-done = bf16[16,1,37,1,3,128]{5,2,4,3,1,0:T(8,128)(2,1)S(1)} async-done(((bf16[16,1,37,1,3,128]{5,2,4,3,1,0:T(8,128)(2,1)}), bf16[16,1,37,1,3,128]{5,2,4,3,1,0:T(8,128)(2,1)S(1)}, u32[]{:S(2)}, u32[]{:S(2)}) %all-to-all-start) | async-done | bytes 454688 | tf_op jit(solution)/shard_map/all_to_all | solution.py:62
  40.2 0.8 %copy.33 = bf16[3,37,16,128]{3,2,1,0:T(8,128)(2,1)} copy(bf16[3,37,16,128]{3,1,0,2:T(8,128)(2,1)S(1)} %bitcast.93) | data formatting | bytes 909312
  (6 shorter events, 0.1 us)
Async XLA Ops:
  0.6 6.4 %copy-start = (bf16[1,137,2048]{2,1,0:T(8,128)(2,1)S(1)}, bf16[1,137,2048]{2,1,0:T(8,128)(2,1)}, u32[]{:S(2)}) copy-start(bf16[1,137,2048]{2,1,0:T(8,128)(2,1)} %param.5) | copy-start | bytes 1683460
  7.1 1.0 %copy-start.1 = (s32[2048]{0:T(1024)S(1)}, s32[2048]{0:T(1024)}, u32[]{:S(2)}) copy-start(s32[2048]{0:T(1024)} %param.6) | copy-start | bytes 24580
  19.1 21.1 %all-to-all-start = ((bf16[16,1,37,1,3,128]{5,2,4,3,1,0:T(8,128)(2,1)}), bf16[16,1,37,1,3,128]{5,2,4,3,1,0:T(8,128)(2,1)S(1)}, u32[]{:S(2)}, u32[]{:S(2)}) async-start(bf16[16,1,37,1,3,128]{5,2,4,3,1,0:T(8,128)(2,1)} %constant_dynamic-update-slice_fusion), calls=%async_computation | async-start | bytes 983040 | tf_op jit(solution)/shard_map/all_to_all | solution.py:62
